TPU v7x, 256 devices: a whole 4x4x8 slice. The times are simulated.
256 devices in a mesh: field: 32 (over z, x), vrow: 2 (over core), vcol: 4 (over y).
Axes of the slice: x: 4, y: 4, z: 8, core: 2. Of those that a mesh axis runs over, the one named last changes fastest.
Arguments:
- blocks: bfloat16 [1024, 192, 2, 256], P(('vrow', 'vcol'), 'field'), may hold values from 0 to 1
- block_ids: int32 [8, 32, 6], P(('vrow', 'vcol'), 'field'), may hold values from 0 to 11, as said below
- block_counts: int32 [8, 32], P(('vrow', 'vcol'), 'field'), may hold values from 1 to 6, as said below
Outputs:
- tables: float32 [1024, 2, 2, 4, 2, 128], P(('vrow', 'field'), None, None, 'vcol')
Inputs may be any that keep to these rules, and one draw needn't show every extreme that they name: `block_ids`: within each row of the last dimension the entries are distinct. `block_counts`: 6 is reached in every draw.
All inputs are finite; a program needn't handle non-finite values.
Results may differ from a plain program's by a relative error of at most 0.0003.
Values may be sent and summed in bfloat16 or wider, within the bound.
No kernel may reach another device: no remote copies, remote signals or barrier semaphores. Data moves between devices by JAX's collectives and lax.ppermute only.
A program may use at most 64 MiB of HBM per device.

v0:
```python
import math
import jax
import jax.numpy as jnp
from jax import lax
from jax.sharding import PartitionSpec as P

SBLK = 12
BLOCK = 256


def side_by_side(arrays, axis, dim, along):
    widths = [math.prod(a.shape[along:]) for a in arrays]
    both = jnp.concatenate(
        [a.reshape(*a.shape[:along], w) for a, w in zip(arrays, widths)], axis=along
    )
    out = lax.all_gather(both, axis, axis=dim, tiled=True)
    parts = jnp.split(out, [sum(widths[:k]) for k in range(1, len(widths))], axis=along)
    return tuple((b.reshape(*out.shape[:along], *a.shape[along:]) for a, b in zip(arrays, parts)))


def split_up(array, dim, length):
    dims = array.shape
    parts = array.reshape(*dims[:dim], length, dims[dim] // length, *dims[dim + 1 :])
    return jnp.moveaxis(parts, dim, 0)


def sent_and_summed(array, axis, dim):
    length = lax.axis_size(axis)
    parts = lax.all_to_all(split_up(array, dim, length), axis, 0, 0, tiled=True)
    return jnp.sum(parts, axis=0)


def expand(blocks, block_ids, block_counts):
    shards = block_ids.shape[0]
    occ = block_ids.shape[-1]
    shaped = blocks.reshape(shards, blocks.shape[0] // shards, occ, 2, blocks.shape[-1])
    slots = jnp.arange(occ, dtype=jnp.int32)
    live = slots[None, :] < block_counts[:, 0][:, None]
    onehot = (block_ids[:, 0, :, None] == jnp.arange(SBLK, dtype=jnp.int32)[None, None, :]) & live[
        ..., None
    ]
    dense = jnp.einsum(
        "sok,svocx->svkcx", onehot.astype(jnp.bfloat16), shaped, preferred_element_type=jnp.float32
    )
    return dense.astype(jnp.bfloat16).reshape(blocks.shape[0], SBLK, 2, blocks.shape[-1])


def on_device(blocks, block_ids, block_counts):
    row_data, row_ids, row_counts = (
        lax.all_gather(blocks, "vcol", axis=0, tiled=True),
        *side_by_side((block_ids, block_counts), "vcol", 0, 2),
    )
    rows = expand(row_data, row_ids, row_counts)
    col_data, col_ids, col_counts = (
        lax.all_gather(blocks, "vrow", axis=0, tiled=True),
        *side_by_side((block_ids, block_counts), "vrow", 0, 2),
    )
    columns = expand(col_data, col_ids, col_counts)
    groups = lax.axis_size("vrow")
    columns = columns.reshape(groups, columns.shape[0] // groups, SBLK, 2, columns.shape[-1])
    fields = lax.axis_size("field")
    term = jnp.einsum("ikcx,rjkdx->icrdj", rows, columns, preferred_element_type=jnp.float32)
    summed = sent_and_summed(term[:, :, :, None], "field", 0)
    return summed / (fields * SBLK * BLOCK)


def solution(mesh):
    placed = (
        P(("vrow", "vcol"), "field", None, None),
        P(("vrow", "vcol"), "field", None),
        P(("vrow", "vcol"), "field"),
    )
    return jax.shard_map(
        on_device,
        mesh=mesh,
        in_specs=placed,
        out_specs=P(("vrow", "field"), None, None, "vcol", None, None),
        check_vma=False,
    )
```

profile of v0, /device:TPU:2, one launch (start us, length us, event | category | flops | bytes accessed | tf_op | source)
XLA Modules:
  0.0 164.3 jit_solution(4973293619530026705)
XLA Ops:
  6.5 0.0 all-gather.3.cloned.1.call-start
  6.5 0.7 all-gather.3.cloned.1.call-update
  7.3 0.0 all-gather.5.cloned.1.call-start
  7.3 0.7 all-gather.5.cloned.1.call-update
  8.7 0.7 pad_add_fusion
  9.4 1.8 %all_gather.12 = s32[2,1,7]{2,1,0:T(1,128)S(1)} all-gather(s32[1,1,7]{2,1,0:T(1,128)S(1)} %pad_add_fusion), channel_id=1, replica_groups=mesh['field'=32,'vrow'=2,'vcol'=4] {'vrow'}, dimensions={0}, use_global_device_ids=true | all-gather | bytes 84 | tf_op jit(solution)/shard_map/all_gather | solution.py:16
  11.2 10.0 %all_gather.14 = s32[4,1,7]{2,1,0:T(1,128)S(1)} all-gather(s32[1,1,7]{2,1,0:T(1,128)S(1)} %pad_add_fusion), channel_id=1, replica_groups=mesh['field'=32,'vrow'=2,'vcol'=4] {'vcol'}, dimensions={0}, use_global_device_ids=true | all-gather | bytes 140 | tf_op jit(solution)/shard_map/all_gather | solution.py:16
  21.1 0.2 slice_reduce_fusion.1
  21.3 0.2 slice_reduce_fusion
  21.6 0.1 iota_compare_fusion.2
  21.6 0.1 iota_compare_fusion.3
  21.7 5.5 %all-gather.3.cloned.1.call-done = bf16[256,6,2,256]{3,2,1,0:T(2,128)(2,1)} async-done(((bf16[128,6,2,256]{3,2,1,0:T(2,128)(2,1)}), bf16[256,6,2,256]{3,2,1,0:T(2,128)(2,1)}) %all-gather.3.cloned.1.call-update) | async-done | bytes 1572880 | tf_op jit(solution)/shard_map/all_gather | solution.py:55
  27.2 1.9 %copy.9 = bf16[256,6,2,256]{3,1,2,0:T(8,128)(2,1)S(1)} copy(bf16[256,6,2,256]{3,2,1,0:T(2,128)(2,1)} %all-gather.3.cloned.1.call-done) | data formatting | bytes 3145728 | tf_op jit(solution)/shard_map/all_gather | solution.py:55
  29.1 3.1 %convert_bitcast_fusion = bf16[2,128,12,2,256,1]{4,2,3,1,0,5:T(8,128)(2,1)} fusion(bf16[2,128,6,2,256]{4,2,3,1,0:T(8,128)(2,1)S(1)} %bitcast.39, s32[2,6]{1,0:T(2,128)S(1)} %bitcast.42, pred[2,6]{1,0:T(4,128)(4,1)S(1)} %iota_compare_fusion.3), kind=kOutput, calls=%fused_computation.3 | convolution fusion | flops 20447520 | bytes 4718652 | tf_op jit(solution)/shard_map/sok,svocx->svkcx/dot_general | solution.py:42
  32.2 40.3 %all-gather.5.cloned.1.call-done = bf16[512,6,2,256]{3,2,1,0:T(2,128)(2,1)} async-done(((bf16[128,6,2,256]{3,2,1,0:T(2,128)(2,1)}), bf16[512,6,2,256]{3,2,1,0:T(2,128)(2,1)}) %all-gather.5.cloned.1.call-update) | async-done | bytes 3145744 | tf_op jit(solution)/shard_map/all_gather | solution.py:50
  72.4 2.9 %copy.10 = bf16[512,6,2,256]{3,1,2,0:T(8,128)(2,1)S(1)} copy(bf16[512,6,2,256]{3,2,1,0:T(2,128)(2,1)} %all-gather.5.cloned.1.call-done) | data formatting | bytes 6291456 | tf_op jit(solution)/shard_map/all_gather | solution.py:50
  75.3 0.0 copy-start
  75.3 4.4 %convolution_convert_fusion = bf16[4,12,128,2,256]{4,1,3,2,0:T(8,128)(2,1)S(1)} fusion(bf16[4,128,6,2,256]{4,2,3,1,0:T(8,128)(2,1)S(1)} %bitcast.37, s32[4,6]{1,0:T(4,128)S(1)} %bitcast.41, pred[4,6]{1,0:T(4,128)(4,1)S(1)} %iota_compare_fusion.2), kind=kOutput, calls=%fused_computation | convolution fusion | flops 40895040 | bytes 9437304 | tf_op jit(solution)/shard_map/sok,svocx->svkcx/dot_general | solution.py:42
  79.8 0.0 copy-done
  79.8 14.4 %fusion.3 = f32[512,2,2,2,128]{0,4,1,3,2:T(8,128)} fusion(bf16[512,12,2,256,1,1]{3,1,2,0,5,4:T(8,128)(2,1)S(1)} %bitcast.38, bf16[2,128,12,2,256,1]{4,2,3,1,0,5:T(8,128)(2,1)S(1)} %copy-done), kind=kOutput, calls=%fused_computation.5 | convolution fusion | flops 3221225472 | bytes 11534336 | tf_op jit(solution)/shard_map/ikcx,rjkdx->icrdj/dot_general | solution.py:62
  94.2 1.9 %copy.13 = f32[512,2,2,2,128]{4,0,3,2,1:T(8,128)S(1)} copy(f32[512,2,2,2,128]{0,4,1,3,2:T(8,128)} %fusion.3) | data formatting | bytes 4194304 | tf_op jit(solution)/shard_map/ikcx,rjkdx->icrdj/transpose | solution.py:62
  96.1 0.3 copy.14
  96.3 60.3 %all_to_all.5 = f32[32,16,2,2,1,2,128]{6,1,5,3,2,4,0:T(8,128)S(1)} all-to-all(f32[32,16,2,2,1,2,128]{6,1,5,3,2,4,0:T(8,128)S(1)} %copy.14), channel_id=1, replica_groups=mesh['field'=32,'vrow'=2,'vcol'=4] {'field'}, dimensions={0} | all-to-all | bytes 4194304 | tf_op jit(solution)/shard_map/all_to_all | solution.py:29
  156.6 0.1 reduce_sum.9
  156.8 0.7 copy.16
  (1 shorter events, 0.0 us)
Async XLA Ops:
  6.5 20.7 %all-gather.3.cloned.1.call-start = ((), (), s32[]{:S(2)}) async-start(), calls=%async_computation.1 | async-start | bytes 2359296 | tf_op jit(solution)/shard_map/all_gather | solution.py:55
  7.3 65.2 %all-gather.5.cloned.1.call-start = ((), (), s32[]{:S(2)}) async-start(), calls=%async_computation.2 | async-start | bytes 3932160 | tf_op jit(solution)/shard_map/all_gather | solution.py:50
  75.3 4.5 %copy-start = (bf16[2,128,12,2,256,1]{4,2,3,1,0,5:T(8,128)(2,1)S(1)}, bf16[2,128,12,2,256,1]{4,2,3,1,0,5:T(8,128)(2,1)}, u32[]{:S(2)}) copy-start(bf16[2,128,12,2,256,1]{4,2,3,1,0,5:T(8,128)(2,1)} %convert_bitcast_fusion) | copy-start | bytes 9437188
Sparse Core Ops, SparseCore 0:
  9.1 18.0 all-gather.2
  29.1 43.3 all-gather.4
where the time goes:
time: 165 us; the launch traced here: 164 us
  blocking collectives  72.1 us (44%)
  waiting for transfers between devices  47.2 us (29%)
  matrix products  21.9 us (13%)
  between operations  14.1 us (9%)
  local copies, waits for them, and re-layouts  7.99 us (5%)
    all_to_all x1, blocking collectives, sent_and_summed(): parts = lax.all_to_all(split_up(array, dim, length), axis, 0, 0, tiled=True)  60.3 us
    all_gather x1, waiting for transfers between devices, on_device(): lax.all_gather(blocks, 'vcol', axis=0, tiled=True)  40.3 us
    dot_general x1, matrix products, on_device(): jnp.einsum('ikcx,rjkdx->icrdj', rows, columns, preferred_element_type=jnp...  14.4 us
    all_gather x2, blocking collectives, side_by_side(): out = lax.all_gather(both, axis, axis=dim, tiled=True)  11.8 us
    dot_general x2, matrix products, expand(): jnp.einsum('sok,svocx->svkcx', onehot.astype(jnp.bfloat16), shaped, prefe...  7.51 us
    all_gather x1, waiting for transfers between devices, on_device(): lax.all_gather(blocks, 'vrow', axis=0, tiled=True)  5.53 us
  transfers between devices with their start and end apart: 2, of which 2 were waited for; matrix products, arithmetic and copies ran while one was open for 4% of the time, Pallas kernels for 0%

commit v1 on v0

--- a/solution.py
+++ b/solution.py
@@ -6,6 +6,27 @@
 
 SBLK = 12
 BLOCK = 256
+
+
+def collect(array, axis, dim):
+    size, index, width = (lax.axis_size(axis), lax.axis_index(axis), array.shape[dim])
+    ahead = [(i, (i + 1) % size) for i in range(size)]
+    backward = [(i, (i - 1) % size) for i in range(size)]
+    out = jnp.zeros((*array.shape[:dim], size * width, *array.shape[dim + 1 :]), array.dtype)
+    out = lax.dynamic_update_slice_in_dim(out, array, index * width, axis=dim)
+    from_left = from_right = array
+    halfway = size // 2
+    for step in range(1, halfway + 1):
+        from_left = lax.ppermute(from_left, axis, ahead)
+        out = lax.dynamic_update_slice_in_dim(
+            out, from_left, (index - step) % size * width, axis=dim
+        )
+        if step < size - halfway:
+            from_right = lax.ppermute(from_right, axis, backward)
+            out = lax.dynamic_update_slice_in_dim(
+                out, from_right, (index + step) % size * width, axis=dim
+            )
+    return out
 
 
 def side_by_side(arrays, axis, dim, along):
@@ -47,7 +68,7 @@
 
 def on_device(blocks, block_ids, block_counts):
     row_data, row_ids, row_counts = (
-        lax.all_gather(blocks, "vcol", axis=0, tiled=True),
+        collect(blocks, "vcol", 0),
         *side_by_side((block_ids, block_counts), "vcol", 0, 2),
     )
     rows = expand(row_data, row_ids, row_counts)

time: 165 us -> 151 us (0.915)
  waiting for transfers between devices: 47.2 us -> 15.8 us
  blocking collectives: 72.1 us -> 79.8 us
  local copies, waits for them, and re-layouts: 7.99 us -> 12.3 us
  starting transfers between devices: 0.04 us -> 3.26 us
  matrix products: 21.9 us -> 24.2 us
    all_gather x1 -> x0, waiting for transfers between devices: 40.3 us -> none  [on_device(): lax.all_gather(blocks, 'vcol', axis=0, tiled=True)]
    ppermute x0 -> x3, waiting for transfers between devices: none -> 15.8 us  [the longest x2 15.8 us: collect(): from_left = lax.ppermute(from_left, axis, ahead)]
    all_gather x2, blocking collectives: 11.8 us -> 20.7 us  [side_by_side(): out = lax.all_gather(both, axis, axis=dim, tiled=True)]
    all_gather x1, waiting for transfers between devices: 5.53 us -> 0.01 us  [on_device(): lax.all_gather(blocks, 'vrow', axis=0, tiled=True)]
    dynamic_update_slice x0 -> x4, local copies, waits for them, and re-layouts: none -> 4.82 us  [the longest x2 2.36 us: collect(): lax.dynamic_update_slice_in_dim(out, from_left, (index - step) % size * w...]
    ppermute x0 -> x3, starting transfers between devices: none -> 3.25 us  [the longest x1 1.66 us: collect(): from_right = lax.ppermute(from_right, axis, backward)]
    all_gather x1 -> x0, local copies, waits for them, and re-layouts: 2.87 us -> none  [on_device(): lax.all_gather(blocks, 'vcol', axis=0, tiled=True)]
    dot_general x2, matrix products: 7.51 us -> 9.82 us  [expand(): jnp.einsum('sok,svocx->svkcx', onehot.astype(jnp.bfloat16), shaped, prefe...]
  transfers between devices with their start and end apart: 2 -> 4, of which waited for: 2 -> 1; matrix products, arithmetic and copies ran while one was open for 4% -> 11% of each run, Pallas kernels for 0% -> 0%
where the time goes in v1:
time: 151 us
  blocking collectives  79.8 us (53%)
  matrix products  24.2 us (16%)
  waiting for transfers between devices  15.8 us (10%)
  between operations  14.2 us (9%)
  local copies, waits for them, and re-layouts  12.3 us (8%)
  starting transfers between devices  3.26 us (2%)
    all_to_all x1, blocking collectives, sent_and_summed(): parts = lax.all_to_all(split_up(array, dim, length), axis, 0, 0, tiled=True)  59.1 us
    all_gather x2, blocking collectives, side_by_side(): out = lax.all_gather(both, axis, axis=dim, tiled=True)  20.7 us
    ppermute x2, waiting for transfers between devices, collect(): from_left = lax.ppermute(from_left, axis, ahead)  15.8 us
    dot_general x1, matrix products, on_device(): jnp.einsum('ikcx,rjkdx->icrdj', rows, columns, preferred_element_type=jnp...  14.4 us
    dot_general x2, matrix products, expand(): jnp.einsum('sok,svocx->svkcx', onehot.astype(jnp.bfloat16), shaped, prefe...  9.82 us
  transfers between devices with their start and end apart: 4, of which 1 were waited for; matrix products, arithmetic and copies ran while one was open for 11% of the time, Pallas kernels for 0%

profile of v1, /device:TPU:2, one launch (start us, length us, event | category | flops | bytes accessed | tf_op | source)
XLA Modules:
  0.0 150.6 jit_solution(2258951376881681822)
XLA Ops:
  6.5 0.0 copy-start.1
  6.5 0.0 all-gather.2.cloned.1.call-start
  6.5 1.6 %collective-permute-start = (bf16[128,6,2,256]{3,2,1,0:T(2,128)(2,1)}, bf16[128,6,2,256]{3,2,1,0:T(2,128)(2,1)S(1)}, u32[]{:S(2)}, u32[]{:S(2)}) collective-permute-start(bf16[128,6,2,256]{3,2,1,0:T(2,128)(2,1)} %param.3), channel_id=1, source_target_pairs={{0,1},{1,2},{2,3},{3,0},{4,5},{5,6},{6,7},{7,4},{8,9},{9,10},{10,1... | collective-permute-start | bytes 2359304 | tf_op jit(solution)/shard_map/ppermute | solution.py:20
  8.1 1.7 %collective-permute-start.1 = (bf16[128,6,2,256]{3,2,1,0:T(2,128)(2,1)}, bf16[128,6,2,256]{3,2,1,0:T(2,128)(2,1)S(1)}, u32[]{:S(2)}, u32[]{:S(2)}) collective-permute-start(bf16[128,6,2,256]{3,2,1,0:T(2,128)(2,1)} %param.3), channel_id=1, source_target_pairs={{0,3},{1,0},{2,1},{3,2},{4,7},{5,4},{6,5},{7,6},{8,11},{9,8},{10,9... | collective-permute-start | bytes 2359304 | tf_op jit(solution)/shard_map/ppermute | solution.py:25
  10.4 0.7 pad_add_fusion
  11.2 0.0 all-gather.2.cloned.1.call-update
  11.2 1.8 %all_gather.9 = s32[2,1,7]{2,1,0:T(1,128)S(1)} all-gather(s32[1,1,7]{2,1,0:T(1,128)S(1)} %pad_add_fusion), channel_id=1, replica_groups=mesh['field'=32,'vrow'=2,'vcol'=4] {'vrow'}, dimensions={0}, use_global_device_ids=true | all-gather | bytes 84 | tf_op jit(solution)/shard_map/all_gather | solution.py:37
  13.0 18.9 %all_gather.11 = s32[4,1,7]{2,1,0:T(1,128)S(1)} all-gather(s32[1,1,7]{2,1,0:T(1,128)S(1)} %pad_add_fusion), channel_id=1, replica_groups=mesh['field'=32,'vrow'=2,'vcol'=4] {'vcol'}, dimensions={0}, use_global_device_ids=true | all-gather | bytes 140 | tf_op jit(solution)/shard_map/all_gather | solution.py:37
  31.9 0.2 slice_reduce_fusion
  32.1 2.3 %broadcast_in_dim.2 = bf16[512,6,2,256]{3,1,2,0:T(8,128)(2,1)} broadcast(bf16[]{:T(256)} %constant.32.clone.1), dimensions={} | broadcast | bytes 3145730 | tf_op jit(solution)/shard_map/broadcast_in_dim | solution.py:15
  34.4 0.0 copy-done.1
  34.4 1.3 copy_dynamic-update-slice_fusion.3
  35.7 0.1 iota_compare_fusion.2
  35.7 0.0 collective-permute-done
  35.7 0.0 collective-permute-start.2
  35.8 0.2 slice_reduce_fusion.1
  36.0 0.1 iota_compare_fusion.3
  36.1 1.2 copy_dynamic-update-slice_fusion.2
  37.3 0.0 collective-permute-done.1
  37.3 1.2 copy_dynamic-update-slice_fusion.1
  38.5 15.8 %collective-permute-done.2 = bf16[128,6,2,256]{3,2,1,0:T(2,128)(2,1)S(1)} collective-permute-done((bf16[128,6,2,256]{3,2,1,0:T(2,128)(2,1)S(1)}, bf16[128,6,2,256]{3,2,1,0:T(2,128)(2,1)S(1)}, u32[]{:S(2)}, u32[]{:S(2)}) %collective-permute-start.2) | collective-permute-done | bytes 786464 | tf_op jit(solution)/shard_map/ppermute | solution.py:20
  54.2 1.2 copy_dynamic-update-slice_fusion
  55.4 7.9 %convolution_convert_fusion = bf16[4,128,2,256,12]{3,4,2,1,0:T(8,128)(2,1)} fusion(bf16[4,128,6,2,256]{4,2,3,1,0:T(8,128)(2,1)} %bitcast.7, s32[4,6]{1,0:T(4,128)S(1)} %bitcast.40, pred[4,6]{1,0:T(4,128)(4,1)S(1)} %iota_compare_fusion.2), kind=kOutput, calls=%fused_computation | convolution fusion | flops 40895040 | bytes 9437304 | tf_op jit(solution)/shard_map/sok,svocx->svkcx/dot_general | solution.py:63
  63.3 0.0 all-gather.2.cloned.1.call-done
  63.3 0.0 copy-start
  63.3 2.0 %copy.15 = bf16[256,6,2,256]{3,1,2,0:T(8,128)(2,1)S(1)} copy(bf16[256,6,2,256]{3,2,1,0:T(2,128)(2,1)} %all-gather.2.cloned.1.call-done) | data formatting | bytes 3145728 | tf_op jit(solution)/shard_map/all_gather | solution.py:76
  65.3 2.0 %convert_bitcast_fusion = bf16[2,128,12,2,256,1]{4,2,3,1,0,5:T(8,128)(2,1)S(1)} fusion(bf16[2,128,6,2,256]{4,2,3,1,0:T(8,128)(2,1)S(1)} %bitcast.38, s32[2,6]{1,0:T(2,128)S(1)} %bitcast.41, pred[2,6]{1,0:T(4,128)(4,1)S(1)} %iota_compare_fusion.3), kind=kOutput, calls=%fused_computation.3 | convolution fusion | flops 20447520 | bytes 4718652 | tf_op jit(solution)/shard_map/sok,svocx->svkcx/dot_general | solution.py:63
  67.2 0.0 copy-done
  67.3 14.4 %fusion.3 = f32[512,2,2,2,128]{0,4,1,3,2:T(8,128)} fusion(bf16[512,12,2,256,1,1]{3,1,2,0,5,4:T(8,128)(2,1)S(1)} %bitcast.37, bf16[2,128,12,2,256,1]{4,2,3,1,0,5:T(8,128)(2,1)S(1)} %convert_bitcast_fusion), kind=kOutput, calls=%fused_computation.5 | convolution fusion | flops 3221225472 | bytes 11534336 | tf_op jit(solution)/shard_map/ikcx,rjkdx->icrdj/dot_general | solution.py:83
  81.6 1.9 %copy.22 = f32[512,2,2,2,128]{4,0,3,2,1:T(8,128)S(1)} copy(f32[512,2,2,2,128]{0,4,1,3,2:T(8,128)} %fusion.3) | data formatting | bytes 4194304 | tf_op jit(solution)/shard_map/ikcx,rjkdx->icrdj/transpose | solution.py:83
  83.6 0.3 copy.23
  83.8 59.1 %all_to_all.5 = f32[32,16,2,2,1,2,128]{6,1,5,3,2,4,0:T(8,128)S(1)} all-to-all(f32[32,16,2,2,1,2,128]{6,1,5,3,2,4,0:T(8,128)S(1)} %copy.23), channel_id=1, replica_groups=mesh['field'=32,'vrow'=2,'vcol'=4] {'field'}, dimensions={0} | all-to-all | bytes 4194304 | tf_op jit(solution)/shard_map/all_to_all | solution.py:50
  142.9 0.1 reduce_sum.9
  143.0 0.7 copy.25
  (1 shorter events, 0.0 us)
Async XLA Ops:
  6.5 27.9 %copy-start.1 = (bf16[128,6,2,256]{3,2,1,0:T(2,128)(2,1)S(1)}, bf16[128,6,2,256]{3,2,1,0:T(2,128)(2,1)}, u32[]{:S(2)}) copy-start(bf16[128,6,2,256]{3,2,1,0:T(2,128)(2,1)} %param.3) | copy-start | bytes 2359300
  6.5 56.7 %all-gather.2.cloned.1.call-start = ((), (), s32[]{:S(2)}) async-start(), calls=%async_computation.1 | async-start | bytes 2359296 | tf_op jit(solution)/shard_map/all_gather | solution.py:76
  6.5 29.2 %collective-permute-start = (bf16[128,6,2,256]{3,2,1,0:T(2,128)(2,1)}, bf16[128,6,2,256]{3,2,1,0:T(2,128)(2,1)S(1)}, u32[]{:S(2)}, u32[]{:S(2)}) collective-permute-start(bf16[128,6,2,256]{3,2,1,0:T(2,128)(2,1)} %param.3), channel_id=1, source_target_pairs={{0,1},{1,2},{2,3},{3,0},{4,5},{5,6},{6,7},{7,4},{8,9},{9,10},{10,1... | collective-permute-start | bytes 2359304 | tf_op jit(solution)/shard_map/ppermute | solution.py:20
  8.1 29.2 %collective-permute-start.1 = (bf16[128,6,2,256]{3,2,1,0:T(2,128)(2,1)}, bf16[128,6,2,256]{3,2,1,0:T(2,128)(2,1)S(1)}, u32[]{:S(2)}, u32[]{:S(2)}) collective-permute-start(bf16[128,6,2,256]{3,2,1,0:T(2,128)(2,1)} %param.3), channel_id=1, source_target_pairs={{0,3},{1,0},{2,1},{3,2},{4,7},{5,4},{6,5},{7,6},{8,11},{9,8},{10,9... | collective-permute-start | bytes 2359304 | tf_op jit(solution)/shard_map/ppermute | solution.py:25
  35.7 18.5 %collective-permute-start.2 = (bf16[128,6,2,256]{3,2,1,0:T(2,128)(2,1)S(1)}, bf16[128,6,2,256]{3,2,1,0:T(2,128)(2,1)S(1)}, u32[]{:S(2)}, u32[]{:S(2)}) collective-permute-start(bf16[128,6,2,256]{3,2,1,0:T(2,128)(2,1)S(1)} %collective-permute-done), channel_id=1, source_target_pairs={{0,1},{1,2},{2,3},{3,0},{4,5},{5,6},{6,7},{7,4},{8,9},{9,10},{10,1... | collective-permute-start | bytes 2359304 | tf_op jit(solution)/shard_map/ppermute | solution.py:20
  63.3 4.0 %copy-start = (bf16[4,128,2,256,12]{3,4,2,1,0:T(8,128)(2,1)S(1)}, bf16[4,128,2,256,12]{3,4,2,1,0:T(8,128)(2,1)}, u32[]{:S(2)}) copy-start(bf16[4,128,2,256,12]{3,4,2,1,0:T(8,128)(2,1)} %convolution_convert_fusion) | copy-start | bytes 18874372
Sparse Core Ops, SparseCore 0:
  11.3 16.8 all-gather.1
